TPU v7x, 32 devices: a whole 2x2x4 slice. The times are simulated.
32 devices in a mesh: samp: 16 (over z, y, x), tgt: 2 (over core).
Axes of the slice: x: 2, y: 2, z: 4, core: 2. Of those that a mesh axis runs over, the one named last changes fastest.
Arguments:
- samples: bfloat16 [3072, 128], P('samp'), may hold values from -6 to 6
- omega: bfloat16 [128, 4096], replicated, may hold values from -0.5 to 0.5
- phase: float32 [4096], replicated, may hold values from -3.140625 to 3.140625
- right_side: float32 [4096, 512], P('samp', 'tgt'), may hold values from -6 to 6
Outputs:
- weights: float32 [4096, 512], P('samp', 'tgt')
All inputs are finite; a program needn't handle non-finite values.
Results may differ from a plain program's by a relative error of at most 0.011.
The roundings to bfloat16 on the way count: a program that leaves them out, or rounds other values in their place, can miss the bound.
Values may be sent and summed in bfloat16 or wider, within the bound.
No kernel may reach another device: no remote copies, remote signals or barrier semaphores. Data moves between devices by JAX's collectives and lax.ppermute only.
A program may use at most 128 MiB of HBM per device.

v0:
```python
import math

import jax
import jax.numpy as jnp
from jax import lax
from jax.sharding import PartitionSpec as P

ITERS = 2


ridge = 1.0


def precise_dot(left_matrix, right_matrix):
    return jnp.dot(left_matrix, right_matrix, precision=lax.Precision.HIGHEST)


def spd_solve(gram_matrix, rhs_matrix):
    factor = jnp.linalg.cholesky(gram_matrix)
    return jax.scipy.linalg.cho_solve((factor, True), rhs_matrix)


def cosine_block(samples, omega, phase, first_row, row_count):
    omega_cols = lax.dynamic_slice_in_dim(omega, first_row, row_count, 1)
    phase_cols = lax.dynamic_slice_in_dim(phase, first_row, row_count, 0)
    preact = jnp.dot(samples, omega_cols, preferred_element_type=jnp.float32) + phase_cols
    return jnp.cos(preact).astype(jnp.bfloat16)


def full_gram(stacked):
    summed = lax.psum(stacked, "samp")
    return lax.all_gather(summed, "tgt", axis=2, tiled=True)


def body(samples, omega, phase, right_side):
    feat_rows, col_count = right_side.shape
    samp_count = lax.axis_size("samp")
    feat_total = omega.shape[1]
    sample_total = samples.shape[0] * samp_count
    col_offset = lax.axis_index("tgt") * col_count
    store_block = math.gcd(feat_total, 512)
    stored = jnp.concatenate(
        [
            cosine_block(samples, omega, phase, index_block * store_block, store_block)
            for index_block in range(feat_total // store_block)
        ],
        axis=1,
    )

    def columns(first_row, row_count):
        return lax.dynamic_slice_in_dim(stored, first_row, row_count, 1)

    resid_all = lax.all_gather(right_side, "tgt", axis=1, tiled=True)
    direction_all = resid_all
    weight_own = jnp.zeros_like(right_side)
    gram_rr = full_gram(precise_dot(resid_all.T, right_side)[None])[0]
    for iteration in range(ITERS):
        direction_own = lax.dynamic_slice_in_dim(direction_all, col_offset, col_count, 1)
        initial = jnp.zeros((samples.shape[0], col_count), jnp.float32)
        shard_piece = lax.all_gather(direction_own.astype(jnp.bfloat16), "samp", axis=0, tiled=True)
        piece_rows = shard_piece.shape[0]
        block_size = math.gcd(piece_rows, 512)

        def project_one_block(index_block, acc_value):
            begin_row = index_block * block_size
            sub_piece = lax.dynamic_slice_in_dim(shard_piece, begin_row, block_size, 0)
            return acc_value + jnp.dot(
                columns(begin_row, block_size), sub_piece, preferred_element_type=jnp.float32
            )

        projected = lax.fori_loop(0, piece_rows // block_size, project_one_block, initial)
        proj_bf = projected.astype(jnp.bfloat16)
        transpose_row_count = feat_rows * lax.axis_size("samp")
        transpose_block_size = math.gcd(transpose_row_count, 512)

        def transpose_one_block(index_block, result):
            begin_row = index_block * transpose_block_size
            feats_block = columns(begin_row, transpose_block_size)
            block_term = lax.dot_general(
                feats_block, proj_bf, (((0,), (0,)), ((), ())), preferred_element_type=jnp.float32
            )
            return lax.dynamic_update_slice_in_dim(result, block_term, begin_row, 0)

        zero_rows = jnp.zeros((transpose_row_count, col_count), jnp.float32)
        summed_image = lax.psum_scatter(
            lax.fori_loop(
                0, transpose_row_count // transpose_block_size, transpose_one_block, zero_rows
            ),
            "samp",
            scatter_dimension=0,
            tiled=True,
        )
        image_own = summed_image / sample_total + ridge * direction_own
        image_all = lax.all_gather(image_own, "tgt", axis=1, tiled=True)
        gram_pq = full_gram(precise_dot(direction_all.T, image_own)[None])[0]
        alpha_coef = spd_solve(gram_pq, gram_rr)
        alpha_own = lax.dynamic_slice_in_dim(alpha_coef, col_offset, col_count, 1)
        weight_own = weight_own + precise_dot(direction_all, alpha_own)
        if iteration + 1 < ITERS:
            resid_all = resid_all - precise_dot(image_all, alpha_coef)
            resid_now = lax.dynamic_slice_in_dim(resid_all, col_offset, col_count, 1)
            gram_new = full_gram(precise_dot(resid_all.T, resid_now)[None])[0]
            beta_coef = spd_solve(gram_rr, gram_new)
            direction_all = resid_all + precise_dot(direction_all, beta_coef)
            gram_rr = gram_new
    return weight_own


def solution(mesh):
    placed = (P("samp", None), P(), P(), P("samp", "tgt"))
    return jax.shard_map(
        body, mesh=mesh, in_specs=placed, out_specs=P("samp", "tgt"), check_vma=False
    )
```

profile of v0, /device:TPU:0, one launch (start us, length us, event | category | flops | bytes accessed | tf_op | source)
XLA Modules:
  0.0 1215.1 jit_solution(10789328759363507932)
XLA Ops:
  22.8 50.4 %all-gather.7.cloned.1.call-done = bf16[4096,256]{1,0:T(8,128)(2,1)} async-done(((bf16[256,256]{1,0:T(8,128)(2,1)}), bf16[4096,256]{1,0:T(8,128)(2,1)}) %all-gather.7.cloned.1.call-update) | async-done | bytes 2097168 | tf_op jit(solution)/shard_map/all_gather | solution.py:60
  96.3 91.8 %reduce-scatter.3.cloned.1.call-done = f32[256,256]{1,0:T(8,128)} async-done(((f32[4096,256]{1,0:T(8,128)}), f32[256,256]{1,0:T(8,128)}) %reduce-scatter.3.cloned.1.call-update) | async-done | bytes 262160 | tf_op jit(solution)/shard_map/reduce_scatter | solution.py:85
  190.6 114.9 %all-reduce.10.cloned.1.call-done = (f32[1,512,256]{1,2,0:T(8,128)}, f32[1,512,256]{1,2,0:T(8,128)}) async-done(((f32[1,512,256]{1,2,0:T(8,128)}, f32[1,512,256]{1,2,0:T(8,128)}), (f32[1,512,256]{1,2,0:T(8,128)}, f32[1,512,256]{1,2,0:T(8,128)})) %all-reduce.10.cloned.1.call-update) | async-done | bytes 1048592 | tf_op jit(solution)/shard_map/psum | solution.py:31
  320.1 11.7 cholesky.374
  344.3 11.7 cholesky.393
  367.6 11.7 cholesky.414
  391.3 11.7 cholesky.431
  408.6 12.0 while.64
  420.6 39.3 %custom-call.38 = f32[4,128,128]{1,2,0:T(8,128)S(1)} custom-call(f32[4,128,128]{2,1,0:T(8,128)S(1)} %get-tuple-element.377), custom_call_target="InvertDiagBlocksLowerTriangular" | custom-call | tf_op jit(solution)/shard_map/jit(_cho_solve)/triangular_solve | solution.py:20
  475.0 11.7 cholesky.446
  502.1 12.5 %cholesky.465 = f32[128,128]{1,0:T(8,128)S(1)} custom-call(f32[128,128]{1,0:T(8,128)} %cholesky.603), custom_call_target="Cholesky" | custom-call | tf_op jit(solution)/shard_map/jit(cholesky)/cholesky | solution.py:19
  529.1 12.5 %cholesky.486 = f32[128,128]{1,0:T(8,128)} custom-call(f32[128,128]{1,0:T(8,128)S(1)} %cholesky.608), custom_call_target="Cholesky" | custom-call | tf_op jit(solution)/shard_map/jit(cholesky)/cholesky | solution.py:19
  555.9 12.3 %cholesky.503 = f32[128,128]{1,0:T(8,128)} custom-call(f32[128,128]{1,0:T(8,128)S(1)} %convolution_subtract_fusion.26), custom_call_target="Cholesky" | custom-call | tf_op jit(solution)/shard_map/jit(cholesky)/cholesky | solution.py:19
  578.3 105.3 %all-reduce.6.cloned.1.call-done = f32[1,512,256]{2,1,0:T(8,128)} async-done(((f32[1,512,256]{2,1,0:T(8,128)}), f32[1,512,256]{2,1,0:T(8,128)}) %all-reduce.6.cloned.1.call-update) | async-done | bytes 524304 | tf_op jit(solution)/shard_map/psum | solution.py:31
  684.4 14.8 %while.65 = (s32[]{:T(128)}, f32[512,512]{1,0:T(8,128)}, s32[4,2]{0,1:T(2,128)S(1)}, f32[4,128,128]{2,1,0:T(8,128)}, s32[]{:T(128)}) while((s32[]{:T(128)}, f32[512,512]{1,0:T(8,128)}, s32[4,2]{0,1:T(2,128)S(1)}, f32[4,128,128]{2,1,0:T(8,128)}, s32[]{:T(128)}) %tuple.227), condition=%wide.while_cond.clone, body=%wide.while_body.clone.sunk | while | flops 2 | bytes 132705 | solution.py:20
  699.2 40.8 %custom-call.42 = f32[4,128,128]{1,2,0:T(8,128)} custom-call(f32[4,128,128]{2,1,0:T(8,128)} %get-tuple-element.378), custom_call_target="InvertDiagBlocksLowerTriangular" | custom-call | tf_op jit(solution)/shard_map/jit(_cho_solve)/triangular_solve | solution.py:20
  752.9 59.5 %all-gather.15.cloned.1.call-done = bf16[4096,256]{1,0:T(8,128)(2,1)} async-done(((bf16[256,256]{1,0:T(8,128)(2,1)}), bf16[4096,256]{1,0:T(8,128)(2,1)}) %all-gather.15.cloned.1.call-update) | async-done | bytes 2097168 | tf_op jit(solution)/shard_map/all_gather | solution.py:60
  833.1 94.1 %reduce-scatter.5.cloned.1.call-done = f32[256,256]{1,0:T(8,128)} async-done(((f32[4096,256]{1,0:T(8,128)}), f32[256,256]{1,0:T(8,128)}) %reduce-scatter.5.cloned.1.call-update) | async-done | bytes 262160 | tf_op jit(solution)/shard_map/reduce_scatter | solution.py:85
  929.9 111.0 %all-reduce.8.cloned.1.call-done = f32[1,512,256]{1,2,0:T(8,128)} async-done(((f32[1,512,256]{1,2,0:T(8,128)}), f32[1,512,256]{1,2,0:T(8,128)}) %all-reduce.8.cloned.1.call-update) | async-done | bytes 524304 | tf_op jit(solution)/shard_map/psum | solution.py:31
  1055.6 11.7 cholesky.518
  1079.8 11.7 cholesky.537
  1104.4 11.7 cholesky.558
  1128.1 11.7 cholesky.575
  1155.9 39.3 %custom-call.46 = f32[4,128,128]{1,2,0:T(8,128)S(1)} custom-call(f32[4,128,128]{2,1,0:T(8,128)S(1)} %get-tuple-element.379), custom_call_target="InvertDiagBlocksLowerTriangular" | custom-call | tf_op jit(solution)/shard_map/jit(_cho_solve)/triangular_solve | solution.py:20
  (300 shorter events, 350.7 us)
Async XLA Ops:
  6.5 4.2 copy-start
  6.5 6.5 copy-start.26
  6.5 66.7 %all-gather.7.cloned.1.call-start = ((), (), s32[]{:S(2)}) async-start(), calls=%async_computation.2 | async-start | bytes 2228224 | tf_op jit(solution)/shard_map/all_gather | solution.py:60
  9.9 178.2 %reduce-scatter.3.cloned.1.call-start = ((), (), s32[]{:S(2)}) async-start(), calls=%async_computation.3 | async-start | bytes 4456448 | tf_op jit(solution)/shard_map/reduce_scatter | solution.py:85
  93.9 211.5 %all-reduce.10.cloned.1.call-start = ((), (), s32[]{:S(2)}) async-start(), calls=%async_computation.12 | async-start | bytes 2097152 | tf_op jit(solution)/shard_map/psum | solution.py:31
  190.5 124.4 %all-gather.9.cloned.1.call-start = ((), (), s32[]{:S(2)}) async-start(), calls=%async_computation.4 | async-start | bytes 1572864 | tf_op jit(solution)/shard_map/all_gather | solution.py:32
  305.5 154.5 %all-gather.11.cloned.1.call-start = ((), (), s32[]{:S(2)}) async-start(), calls=%async_computation.5 | async-start | bytes 1572864 | tf_op jit(solution)/shard_map/all_gather | solution.py:32
  307.8 375.8 %all-reduce.6.cloned.1.call-start = ((), (), s32[]{:S(2)}) async-start(), calls=%async_computation.6 | async-start | bytes 1048576 | tf_op jit(solution)/shard_map/psum | solution.py:31
  315.0 2.7 copy-start.9
  459.9 7.9 copy-start.20
  460.0 2.7 copy-start.1
  468.2 3.4 copy-start.21
  568.2 7.6 copy-start.25
  573.2 166.8 %all-gather.13.cloned.1.call-start = ((), (), s32[]{:S(2)}) async-start(), calls=%async_computation.7 | async-start | bytes 1572864 | tf_op jit(solution)/shard_map/all_gather | solution.py:32
  683.6 128.7 %all-gather.15.cloned.1.call-start = ((), (), s32[]{:S(2)}) async-start(), calls=%async_computation.8 | async-start | bytes 2228224 | tf_op jit(solution)/shard_map/all_gather | solution.py:60
  699.2 44.9 %copy-start.6 = (f32[512,512]{1,0:T(8,128)S(1)}, f32[512,512]{1,0:T(8,128)}, u32[]{:S(2)}) copy-start(f32[512,512]{1,0:T(8,128)} %get-tuple-element.842) | copy-start | bytes 3145732
  740.0 5.5 copy-start.22
  752.8 174.4 %reduce-scatter.5.cloned.1.call-start = ((), (), s32[]{:S(2)}) async-start(), calls=%async_computation.9 | async-start | bytes 4456448 | tf_op jit(solution)/shard_map/reduce_scatter | solution.py:85
  833.0 207.9 %copy-start.3 = (f32[128,512]{1,0:T(8,128)S(1)}, f32[128,512]{1,0:T(8,128)}, u32[]{:S(2)}) copy-start(f32[128,512]{1,0:T(8,128)} %copy-done.2) | copy-start | bytes 786436
  833.0 207.9 %copy-start.13 = (f32[128,512]{1,0:T(8,128)S(1)}, f32[128,512]{1,0:T(8,128)}, u32[]{:S(2)}) copy-start(f32[128,512]{1,0:T(8,128)} %copy-done.12) | copy-start | bytes 786436
  833.0 207.9 %copy-start.18 = (f32[128,512]{1,0:T(8,128)S(1)}, f32[128,512]{1,0:T(8,128)}, u32[]{:S(2)}) copy-start(f32[128,512]{1,0:T(8,128)} %fusion.170) | copy-start | bytes 786436
  833.0 207.9 %all-reduce.8.cloned.1.call-start = ((), (), s32[]{:S(2)}) async-start(), calls=%async_computation.10 | async-start | bytes 1048576 | tf_op jit(solution)/shard_map/psum | solution.py:31
  929.7 120.8 %all-gather.17.cloned.1.call-start = ((), (), s32[]{:S(2)}) async-start(), calls=%async_computation.11 | async-start | bytes 1572864 | tf_op jit(solution)/shard_map/all_gather | solution.py:32
  1155.9 42.5 %copy-start.8 = (f32[512,512]{1,0:T(8,128)S(1)}, f32[512,512]{1,0:T(8,128)}, u32[]{:S(2)}) copy-start(f32[512,512]{1,0:T(8,128)} %get-tuple-element.844) | copy-start | bytes 3145732
  (14 other events, 19.6 us)
Sparse Core Ops, SparseCore 0:
  10.1 63.1 all-gather.6
  94.0 94.0 reduce-scatter.2
  193.4 111.9 all-reduce.9
  306.8 8.0 all-gather.8
  316.4 10.1 all-gather.10
  573.3 110.2 all-reduce.5
  685.2 8.0 all-gather.12
  752.9 59.3 all-gather.14
  833.1 94.0 reduce-scatter.4
  932.2 108.6 all-reduce.7
  1042.4 8.0 all-gather.16
where the time goes:
time: 1230 us; the launch traced here: 1220 us
  waiting for transfers between devices  643 us (52%)
  other arithmetic  372 us (30%)
  matrix products  111 us (9%)
  local copies, waits for them, and re-layouts  60.6 us (5%)
  between operations  22.3 us (2%)
    psum x3, waiting for transfers between devices, full_gram(): summed = lax.psum(stacked, 'samp')  331 us
    another operation x43, other arithmetic, spd_solve(): factor = jnp.linalg.cholesky(gram_matrix)  243 us
    reduce_scatter x2, waiting for transfers between devices, body(): lax.psum_scatter(lax.fori_loop(0, transpose_row_count // transpose_block_...  186 us
    another operation x8, other arithmetic, spd_solve(): return jax.scipy.linalg.cho_solve((factor, True), rhs_matrix)  124 us
    all_gather x2, waiting for transfers between devices, body(): lax.all_gather(direction_own.astype(jnp.bfloat16), 'samp', axis=0, tiled=...  110 us
    another operation x40, local copies, waits for them, and re-layouts, spd_solve(): return jax.scipy.linalg.cho_solve((factor, True), rhs_matrix)  38.5 us
    another operation x42, matrix products, spd_solve(): return jax.scipy.linalg.cho_solve((factor, True), rhs_matrix)  31.8 us
  transfers between devices with their start and end apart: 11, of which 9 were waited for; matrix products, arithmetic and copies ran while one was open for 18% of the time, Pallas kernels for 0%

commit v1 on v0

v1 whole, which is shorter than its diff:
```python
import functools

import jax
import jax.numpy as jnp
from jax import lax
from jax.experimental import pallas as pl
from jax.experimental.pallas import tpu as pltpu
from jax.sharding import PartitionSpec as P

ITERS = 2
PIVOTS = 4
LANES = 128

ridge = 1.0


def precise_dot(left_matrix, right_matrix):
    return jnp.dot(left_matrix, right_matrix, precision=lax.Precision.HIGHEST)


def tile_inverse(tile):
    size = tile.shape[0]
    lane = lax.broadcasted_iota(jnp.int32, (1, size), 1)
    sub = lax.broadcasted_iota(jnp.int32, (8, size), 0)

    def group(_, mat):
        for first in range(0, 8, PIVOTS):
            spots = list(range(first, first + PIVOTS))
            cols = [jnp.broadcast_to(mat[:, j : j + 1], (size, size)) for j in spots]
            pivot_lanes = (lane >= first) & (lane < first + PIVOTS)
            rows = [
                jnp.where(pivot_lanes, jnp.where(lane == j, 1.0, 0.0), mat[j : j + 1, :]) for j in spots
            ]
            small = [[cols[b][spots[a] : spots[a] + 1, :] for b in range(PIVOTS)] for a in range(PIVOTS)]
            for a in range(PIVOTS):
                scale = 1.0 / small[a][a]
                rows[a] = rows[a] * scale
                small[a] = [v * scale for v in small[a]]
                for c in range(PIVOTS):
                    if c != a:
                        factor = small[c][a]
                        rows[c] = rows[c] - factor * rows[a]
                        small[c] = [
                            small[c][b] - factor * small[a][b] if b > a else small[c][b]
                            for b in range(PIVOTS)
                        ]
            mat = jnp.where(pivot_lanes, 0.0, mat)
            for a in range(PIVOTS):
                mat = mat - cols[a] * rows[a]
            top = mat[:8]
            for a, j in enumerate(spots):
                top = jnp.where(sub == j, rows[a], top)
            mat = jnp.concatenate([top, mat[8:]], axis=0)
        mat = jnp.concatenate([mat[8:], mat[:8]], axis=0)
        return pltpu.roll(mat, size - 8, 1)

    return lax.fori_loop(0, size // 8, group, tile)


def inverse_kernel(gram_ref, out_ref):
    size = gram_ref.shape[0]
    dot = functools.partial(
        jnp.dot, precision=lax.Precision.HIGHEST, preferred_element_type=jnp.float32
    )
    out_ref[...] = gram_ref[...]

    def step(begin):
        inv = tile_inverse(out_ref[pl.ds(begin, LANES), pl.ds(begin, LANES)])
        panel = out_ref[:, pl.ds(begin, LANES)]
        new_rows = dot(inv, out_ref[pl.ds(begin, LANES), :])
        out_ref[...] = out_ref[...] - dot(panel, new_rows)
        out_ref[:, pl.ds(begin, LANES)] = -dot(panel, inv)
        out_ref[pl.ds(begin, LANES), :] = new_rows
        out_ref[pl.ds(begin, LANES), pl.ds(begin, LANES)] = inv

    for begin in range(0, size, LANES):
        step(begin)


def spd_inverse(gram_matrix):
    return pl.pallas_call(
        inverse_kernel,
        out_shape=jax.ShapeDtypeStruct(gram_matrix.shape, jnp.float32),
        name="spd_inverse",
    )(gram_matrix)


def cosine_features(samples, omega, phase):
    preact = jnp.dot(samples, omega, preferred_element_type=jnp.float32) + phase
    return jnp.cos(preact).astype(jnp.bfloat16)


def gram(left, right):
    return lax.dot_general(
        left, right, (((0,), (0,)), ((), ())), preferred_element_type=jnp.float32
    )


def wide_dot(narrow, wide):
    high = wide.astype(jnp.bfloat16)
    low = (wide - high.astype(jnp.float32)).astype(jnp.bfloat16)
    return jnp.dot(narrow, high, preferred_element_type=jnp.float32) + jnp.dot(
        narrow, low, preferred_element_type=jnp.float32
    )


def body(samples, omega, phase, right_side):
    feat_rows, col_count = right_side.shape
    sample_total = samples.shape[0] * lax.axis_size("samp")
    col_offset = lax.axis_index("tgt") * col_count
    row_offset = lax.axis_index("samp") * feat_rows

    def own_columns(whole):
        return lax.dynamic_slice_in_dim(whole, col_offset, col_count, 1)

    def gather_rows(piece):
        return lax.all_gather(piece, "samp", axis=0, tiled=True)

    def gather_columns(piece):
        return lax.all_gather(piece, "tgt", axis=1, tiled=True)

    start_half = gather_rows(right_side.astype(jnp.bfloat16))
    all_samples = gather_rows(samples)
    start_rows = gather_columns(right_side)
    feats_own = cosine_features(samples, omega, phase)
    feats_cols = cosine_features(
        all_samples,
        lax.dynamic_slice_in_dim(omega, row_offset, feat_rows, 1),
        lax.dynamic_slice_in_dim(phase, row_offset, feat_rows, 0),
    )

    def project(direction_half):
        own = jnp.dot(feats_own, direction_half, preferred_element_type=jnp.float32)
        return gather_columns(gather_rows(own.astype(jnp.bfloat16)))

    proj = project(start_half)
    start = gather_columns(start_half)
    gram_rr = gram(start, start)
    inv_rr = spd_inverse(gram_rr)
    gram_pq = ridge * gram_rr + gram(proj, proj) / sample_total
    alpha = precise_dot(spd_inverse(gram_pq), gram_rr)
    image_rows = gram(feats_cols, proj) / sample_total + ridge * start_rows
    resid_rows = start_rows - precise_dot(image_rows, alpha)
    resid = gather_columns(gather_rows(own_columns(resid_rows).astype(jnp.bfloat16)))
    gram_new = gram(resid, resid)
    beta = precise_dot(inv_rr, gram_new)
    direction = (resid.astype(jnp.float32) + wide_dot(start, beta)).astype(jnp.bfloat16)
    proj_next = project(own_columns(direction))
    direction_rows = resid_rows + precise_dot(start_rows, beta)
    gram_next = ridge * gram(direction, direction) + gram(proj_next, proj_next) / sample_total
    alpha_next = precise_dot(spd_inverse(gram_next), own_columns(gram_new))
    return precise_dot(start_rows, own_columns(alpha)) + precise_dot(direction_rows, alpha_next)


def solution(mesh):
    placed = (P("samp", None), P(), P(), P("samp", "tgt"))
    return jax.shard_map(
        body, mesh=mesh, in_specs=placed, out_specs=P("samp", "tgt"), check_vma=False
    )
```

time: 1230 us -> 483 us (0.39)
  waiting for transfers between devices: 643 us -> 226 us
  other arithmetic: 372 us -> 1.71 us
  Pallas kernels: 0 us -> 99.6 us
  local copies, waits for them, and re-layouts: 60.6 us -> 4.28 us
  blocking collectives: 4.95 us -> 47.7 us
  matrix products: 111 us -> 81.7 us
    another operation x51 -> x0, other arithmetic: 368 us -> none  [the longest x43 243 us: spd_solve(): factor = jnp.linalg.cholesky(gram_matrix)]
    psum x3 -> x0, waiting for transfers between devices: 331 us -> none  [full_gram(): summed = lax.psum(stacked, 'samp')]
    reduce_scatter x2 -> x0, waiting for transfers between devices: 186 us -> none  [body(): lax.psum_scatter(lax.fori_loop(0, transpose_row_count // transpose_block_...]
    pallas_call x0 -> x3, Pallas kernels: none -> 99.6 us  [spd_inverse(): pl.pallas_call(inverse_kernel, out_shape=jax.ShapeDtypeStruct(gram_matrix...]
    all_gather x6 -> x8, waiting for transfers between devices: 126 us -> 225 us  [the longest x4 222 us: gather_rows(): return lax.all_gather(piece, 'samp', axis=0, tiled=True)]
    another operation x60 -> x0, matrix products: 50 us -> none  [the longest x42 31.8 us: spd_solve(): return jax.scipy.linalg.cho_solve((factor, True), rhs_matrix)]
    another operation x54 -> x0, local copies, waits for them, and re-layouts: 43.9 us -> none  [the longest x40 38.5 us: spd_solve(): return jax.scipy.linalg.cho_solve((factor, True), rhs_matrix)]
    all_gather x2, blocking collectives: 4.95 us -> 47.7 us  [the longest x1 45.6 us: gather_rows(): return lax.all_gather(piece, 'samp', axis=0, tiled=True)]
  transfers between devices with their start and end apart: 11 -> 8, of which waited for: 9 -> 5; matrix products, arithmetic and copies ran while one was open for 18% -> 6% of each run, Pallas kernels for 0% -> 7%
where the time goes in v1:
time: 483 us; the launch traced here: 475 us
  waiting for transfers between devices  226 us (47%)
  Pallas kernels  99.6 us (21%)
  matrix products  81.7 us (17%)
  blocking collectives  47.7 us (10%)
  between operations  14.1 us (3%)
    all_gather x4, waiting for transfers between devices, gather_rows(): return lax.all_gather(piece, 'samp', axis=0, tiled=True)  222 us
    pallas_call x3, Pallas kernels, spd_inverse(): pl.pallas_call(inverse_kernel, out_shape=jax.ShapeDtypeStruct(gram_matrix...  99.6 us
    all_gather x1, blocking collectives, gather_rows(): return lax.all_gather(piece, 'samp', axis=0, tiled=True)  45.6 us
    dot_general x6, matrix products, gram(): lax.dot_general(left, right, (((0,), (0,)), ((), ())), preferred_element_...  44.5 us
    dot_general x7, matrix products, precise_dot(): return jnp.dot(left_matrix, right_matrix, precision=lax.Precision.HIGHEST)  14.2 us
    dot_general x1, matrix products, cosine_features(): preact = jnp.dot(samples, omega, preferred_element_type=jnp.float32) + phase  12.1 us
  transfers between devices with their start and end apart: 8, of which 5 were waited for; matrix products, arithmetic and copies ran while one was open for 6% of the time, Pallas kernels for 7%

profile of v1, /device:TPU:0, one launch (start us, length us, event | category | flops | bytes accessed | tf_op | source)
XLA Modules:
  0.0 475.3 jit_solution(7571739123561206635)
XLA Ops:
  8.3 12.1 %fusion.2 = bf16[192,4096]{1,0:T(8,128)(2,1)S(1)} fusion(bf16[192,128]{1,0:T(8,128)(2,1)} %param.4, bf16[128,4096]{1,0:T(8,128)(2,1)S(1)} %copy-done, f32[4096]{0:T(1024)} %param.6), kind=kOutput, calls=%fused_computation.4 | convolution fusion | flops 202899456 | bytes 2686976 | tf_op jit(solution)/shard_map/dot_general | solution.py:89
  20.5 52.8 %all-gather.9.cloned.1.call-done = bf16[4096,256]{1,0:T(8,128)(2,1)} async-done(((bf16[256,256]{1,0:T(8,128)(2,1)}), bf16[4096,256]{1,0:T(8,128)(2,1)}) %all-gather.9.cloned.1.call-update) | async-done | bytes 2097168 | tf_op jit(solution)/shard_map/all_gather | solution.py:117
  73.3 2.9 convolution_convert_fusion
  76.9 56.1 %all-gather.13.cloned.1.call-done = bf16[3072,256]{1,0:T(8,128)(2,1)} async-done(((bf16[192,256]{1,0:T(8,128)(2,1)}), bf16[3072,256]{1,0:T(8,128)(2,1)}) %all-gather.13.cloned.1.call-update) | async-done | bytes 1572880 | tf_op jit(solution)/shard_map/all_gather | solution.py:117
  133.9 2.2 all_gather.34
  136.1 45.6 %all_gather.35 = bf16[3072,128]{1,0:T(8,128)(2,1)} all-gather(bf16[192,128]{1,0:T(8,128)(2,1)S(1)} %copy-done.13), channel_id=1, replica_groups=mesh['samp'=16,'tgt'=2] {'samp'}, dimensions={0}, use_global_device_ids=true | all-gather | bytes 835584 | tf_op jit(solution)/shard_map/all_gather | solution.py:117
  181.6 5.8 %fusion.30.gram_ref = f32[512,512]{1,0:T(8,128)S(1)} fusion(bf16[4096,512]{1,0:T(8,128)(2,1)} %all-gather.11.cloned.1.call-done), kind=kOutput, calls=%fused_computation.37 | convolution fusion | flops 2147483648 | bytes 5242880 | tf_op jit(solution)/shard_map/dot_general | solution.py:94
  187.5 6.0 %fusion.8.gram_ref = f32[512,512]{1,0:T(8,128)} fusion(f32[512,512]{1,0:T(8,128)S(1)} %fusion.30.gram_ref, bf16[3072,512]{1,0:T(8,128)(2,1)} %all-gather.15.cloned.1.call-done), kind=kOutput, calls=%fused_computation.13 | convolution fusion | flops 1611137024 | bytes 5242880 | tf_op jit(solution)/shard_map/dot_general | solution.py:94
  193.5 33.4 %spd_inverse.3 = f32[512,512]{1,0:T(8,128)} custom-call(f32[512,512]{1,0:T(8,128)} %fusion.8.gram_ref), custom_call_target="tpu_custom_call" | custom-call | tf_op jit(solution)/shard_map/spd_inverse/pallas_call | solution.py:81
  226.9 4.0 fusion.31
  231.0 14.1 %fusion.12 = f32[256,512]{1,0:T(8,128)} fusion(f32[256,512]{1,0:T(8,128)S(1)} %all_gather.34, bf16[3072,512]{1,0:T(8,128)(2,1)} %all-gather.15.cloned.1.call-done, bf16[3072,128]{1,0:T(8,128)(2,1)} %all_gather.35, f32[256]{0:T(256)S(1)} %dynamic_slice.20, bf16[128,4096]{1,0:T(8,128)(2,1)S(1)} %copy-done, s32[]{:T(128)S(6)} %select_n.5), kind=kOutput, calls=%fused_computation.19 | convolution fusion | flops 1008467968 | bytes 5047300 | tf_op jit(solution)/shard_map/dot_general | solution.py:94
  245.0 2.1 convolution_subtract_fusion
  247.9 56.3 %all-gather.17.cloned.1.call-done = bf16[4096,256]{1,0:T(8,128)(2,1)} async-done(((bf16[256,256]{1,0:T(8,128)(2,1)}), bf16[4096,256]{1,0:T(8,128)(2,1)}) %all-gather.17.cloned.1.call-update) | async-done | bytes 2097168 | tf_op jit(solution)/shard_map/all_gather | solution.py:117
  304.3 33.1 %spd_inverse.4 = f32[512,512]{1,0:T(8,128)} custom-call(f32[512,512]{1,0:T(8,128)} %copy-done.4), custom_call_target="tpu_custom_call" | custom-call | tf_op jit(solution)/shard_map/spd_inverse/pallas_call | solution.py:81
  337.5 5.9 %fusion.32 = f32[512,512]{1,0:T(8,128)S(1)} fusion(bf16[4096,512]{1,0:T(8,128)(2,1)} %all-gather.19.cloned.1.call-done), kind=kOutput, calls=%fused_computation.39 | convolution fusion | flops 2147483648 | bytes 5242880 | tf_op jit(solution)/shard_map/dot_general | solution.py:94
  345.3 2.3 fusion.21
  347.7 2.9 fusion
  352.6 2.7 fusion.14
  355.6 56.6 %all-gather.21.cloned.1.call-done = bf16[3072,256]{1,0:T(8,128)(2,1)} async-done(((bf16[192,256]{1,0:T(8,128)(2,1)}), bf16[3072,256]{1,0:T(8,128)(2,1)}) %all-gather.21.cloned.1.call-update) | async-done | bytes 1572880 | tf_op jit(solution)/shard_map/all_gather | solution.py:117
  414.1 6.8 %fusion.34 = f32[512,512]{1,0:T(8,128)} fusion(bf16[4096,512]{1,0:T(8,128)(2,1)} %copy-done.2), kind=kOutput, calls=%fused_computation.41 | convolution fusion | flops 2147483648 | bytes 5242880 | tf_op jit(solution)/shard_map/dot_general | solution.py:94
  420.9 3.0 all-gather.23.cloned.1.call-done
  423.9 5.9 %fusion.9.gram_ref = f32[512,512]{1,0:T(8,128)} fusion(f32[512,512]{1,0:T(8,128)} %fusion.34, bf16[3072,512]{1,0:T(8,128)(2,1)} %all-gather.23.cloned.1.call-done), kind=kOutput, calls=%fused_computation.14 | convolution fusion | flops 1611137024 | bytes 5242880 | tf_op jit(solution)/shard_map/dot_general | solution.py:94
  429.8 33.0 %spd_inverse.5 = f32[512,512]{1,0:T(8,128)} custom-call(f32[512,512]{1,0:T(8,128)} %fusion.9.gram_ref), custom_call_target="tpu_custom_call" | custom-call | tf_op jit(solution)/shard_map/spd_inverse/pallas_call | solution.py:81
  462.8 2.3 fusion.17
  (55 shorter events, 13.1 us)
Async XLA Ops:
  6.5 1.8 copy-start
  6.5 66.7 %all-gather.9.cloned.1.call-start = ((), (), s32[]{:S(2)}) async-start(), calls=%async_computation | async-start | bytes 2228224 | tf_op jit(solution)/shard_map/all_gather | solution.py:117
  8.3 124.8 %all-gather.13.cloned.1.call-start = ((), (), s32[]{:S(2)}) async-start(), calls=%async_computation.2 | async-start | bytes 1671168 | tf_op jit(solution)/shard_map/all_gather | solution.py:117
  20.5 113.4 %copy-start.9 = (bf16[192,4096]{1,0:T(8,128)(2,1)}, bf16[192,4096]{1,0:T(8,128)(2,1)S(1)}, u32[]{:S(2)}) copy-start(bf16[192,4096]{1,0:T(8,128)(2,1)S(1)} %fusion.2) | copy-start | bytes 4718596
  73.3 60.6 %copy-start.12 = (f32[256,256]{1,0:T(8,128)S(1)}, f32[256,256]{1,0:T(8,128)}, u32[]{:S(2)}) copy-start(f32[256,256]{1,0:T(8,128)} %param.7) | copy-start | bytes 786436
  76.1 60.0 %copy-start.13 = (bf16[192,128]{1,0:T(8,128)(2,1)S(1)}, bf16[192,128]{1,0:T(8,128)(2,1)}, u32[]{:S(2)}) copy-start(bf16[192,128]{1,0:T(8,128)(2,1)} %param.4) | copy-start | bytes 147460
  76.1 105.5 %all-gather.11.cloned.1.call-start = ((), (), s32[]{:S(2)}) async-start(), calls=%async_computation.1 | async-start | bytes 6291456 | tf_op jit(solution)/shard_map/all_gather | solution.py:120
  76.9 110.6 %all-gather.15.cloned.1.call-start = ((), (), s32[]{:S(2)}) async-start(), calls=%async_computation.3 | async-start | bytes 4718592 | tf_op jit(solution)/shard_map/all_gather | solution.py:120
  133.1 171.2 %all-gather.17.cloned.1.call-start = ((), (), s32[]{:S(2)}) async-start(), calls=%async_computation.4 | async-start | bytes 2228224 | tf_op jit(solution)/shard_map/all_gather | solution.py:117
  187.5 39.5 %copy-start.4 = (f32[512,512]{1,0:T(8,128)}, f32[512,512]{1,0:T(8,128)S(1)}, u32[]{:S(2)}) copy-start(f32[512,512]{1,0:T(8,128)S(1)} %fusion.30.gram_ref) | copy-start | bytes 3145732
  231.0 14.1 %copy-start.7 = (f32[512,512]{1,0:T(8,128)S(1)}, f32[512,512]{1,0:T(8,128)}, u32[]{:S(2)}) copy-start(f32[512,512]{1,0:T(8,128)} %fusion.31) | copy-start | bytes 3145732
  247.9 89.6 %all-gather.19.cloned.1.call-start = ((), (), s32[]{:S(2)}) async-start(), calls=%async_computation.5 | async-start | bytes 6291456 | tf_op jit(solution)/shard_map/all_gather | solution.py:120
  304.3 107.9 %all-gather.21.cloned.1.call-start = ((), (), s32[]{:S(2)}) async-start(), calls=%async_computation.6 | async-start | bytes 1671168 | tf_op jit(solution)/shard_map/all_gather | solution.py:117
  337.5 6.0 %copy-start.10 = (f32[512,512]{1,0:T(8,128)S(1)}, f32[512,512]{1,0:T(8,128)}, u32[]{:S(2)}) copy-start(f32[512,512]{1,0:T(8,128)} %spd_inverse.4) | copy-start | bytes 3145732
  337.5 7.8 %copy-start.1 = (bf16[4096,512]{1,0:T(8,128)(2,1)S(1)}, bf16[4096,512]{1,0:T(8,128)(2,1)}, u32[]{:S(2)}) copy-start(bf16[4096,512]{1,0:T(8,128)(2,1)} %all-gather.11.cloned.1.call-done) | copy-start | bytes 12582916
  343.4 1.9 copy-start.5
  345.3 2.4 copy-start.3
  350.6 2.0 copy-start.2
  355.3 68.6 %all-gather.23.cloned.1.call-start = ((), (), s32[]{:S(2)}) async-start(), calls=%async_computation.7 | async-start | bytes 4718592 | tf_op jit(solution)/shard_map/all_gather | solution.py:120
  420.9 41.9 %copy-start.6 = (f32[512,512]{1,0:T(8,128)S(1)}, f32[512,512]{1,0:T(8,128)}, u32[]{:S(2)}) copy-start(f32[512,512]{1,0:T(8,128)} %copy-done.5) | copy-start | bytes 3145732
  429.8 35.3 %copy-start.11 = (f32[256,512]{1,0:T(8,128)S(1)}, f32[256,512]{1,0:T(8,128)}, u32[]{:S(2)}) copy-start(f32[256,512]{1,0:T(8,128)} %fusion.11) | copy-start | bytes 1572868
  462.8 3.3 copy-start.8
Sparse Core Ops, SparseCore 0:
  10.1 63.1 all-gather.8
  76.3 56.7 all-gather.12
  134.6 11.4 all-gather.10
  147.5 12.6 all-gather.14
  248.0 56.2 all-gather.16
  305.6 11.5 all-gather.18
  355.4 56.7 all-gather.20
  413.7 10.1 all-gather.22

commit v2 on v1

--- a/solution.py
+++ b/solution.py
@@ -119,8 +119,15 @@
     def gather_columns(piece):
         return lax.all_gather(piece, "tgt", axis=1, tiled=True)
 
-    start_half = gather_rows(right_side.astype(jnp.bfloat16))
-    all_samples = gather_rows(samples)
+    packed = jnp.concatenate(
+        [right_side.astype(jnp.bfloat16), samples.reshape(-1, col_count)], axis=0
+    )
+    packed = gather_rows(packed[None])
+    start_half = packed[:, :feat_rows].reshape(-1, col_count)
+    all_samples = packed[:, feat_rows:].reshape(-1, samples.shape[1])
+    start = gather_columns(start_half)
+    gram_rr = gram(start, start)
+    inv_rr = spd_inverse(gram_rr)
     start_rows = gather_columns(right_side)
     feats_own = cosine_features(samples, omega, phase)
     feats_cols = cosine_features(
@@ -131,12 +138,10 @@
 
     def project(direction_half):
         own = jnp.dot(feats_own, direction_half, preferred_element_type=jnp.float32)
-        return gather_columns(gather_rows(own.astype(jnp.bfloat16)))
+        return gather_rows(own.astype(jnp.bfloat16))
 
-    proj = project(start_half)
-    start = gather_columns(start_half)
-    gram_rr = gram(start, start)
-    inv_rr = spd_inverse(gram_rr)
+    proj_half, inv_rr, feats_cols = lax.optimization_barrier((project(start_half), inv_rr, feats_cols))
+    proj = gather_columns(proj_half)
     gram_pq = ridge * gram_rr + gram(proj, proj) / sample_total
     alpha = precise_dot(spd_inverse(gram_pq), gram_rr)
     image_rows = gram(feats_cols, proj) / sample_total + ridge * start_rows
@@ -145,7 +150,7 @@
     gram_new = gram(resid, resid)
     beta = precise_dot(inv_rr, gram_new)
     direction = (resid.astype(jnp.float32) + wide_dot(start, beta)).astype(jnp.bfloat16)
-    proj_next = project(own_columns(direction))
+    proj_next = gather_columns(project(own_columns(direction)))
     direction_rows = resid_rows + precise_dot(start_rows, beta)
     gram_next = ridge * gram(direction, direction) + gram(proj_next, proj_next) / sample_total
     alpha_next = precise_dot(spd_inverse(gram_next), own_columns(gram_new))

time: 483 us -> 439 us (0.909)
  blocking collectives: 47.7 us -> 2.35 us
  waiting for transfers between devices: 226 us -> 221 us
  local copies, waits for them, and re-layouts: 4.28 us -> 9.14 us
    all_gather x1 -> x0, blocking collectives: 45.6 us -> none  [gather_rows(): return lax.all_gather(piece, 'samp', axis=0, tiled=True)]
    all_gather x4, waiting for transfers between devices: 222 us -> 196 us  [gather_rows(): return lax.all_gather(piece, 'samp', axis=0, tiled=True)]
    all_gather x4, waiting for transfers between devices: 3 us -> 24.7 us  [gather_columns(): return lax.all_gather(piece, 'tgt', axis=1, tiled=True)]
    dot_general x1 -> x2, matrix products: 12.1 us -> 23.8 us  [cosine_features(): preact = jnp.dot(samples, omega, preferred_element_type=jnp.float32) + phase]
    dot_general x6, matrix products: 44.5 us -> 34.2 us  [gram(): lax.dot_general(left, right, (((0,), (0,)), ((), ())), preferred_element_...]
  transfers between devices with their start and end apart: 8 -> 8, of which waited for: 5 -> 7; matrix products, arithmetic and copies ran while one was open for 6% -> 10% of each run, Pallas kernels for 7% -> 8%
where the time goes in v2:
time: 439 us; the launch traced here: 430 us
  waiting for transfers between devices  221 us (50%)
  Pallas kernels  99.3 us (23%)
  matrix products  82.5 us (19%)
  between operations  14.2 us (3%)
  local copies, waits for them, and re-layouts  9.14 us (2%)
    all_gather x4, waiting for transfers between devices, gather_rows(): return lax.all_gather(piece, 'samp', axis=0, tiled=True)  196 us
    pallas_call x3, Pallas kernels, spd_inverse(): pl.pallas_call(inverse_kernel, out_shape=jax.ShapeDtypeStruct(gram_matrix...  99.3 us
    dot_general x6, matrix products, gram(): lax.dot_general(left, right, (((0,), (0,)), ((), ())), preferred_element_...  34.2 us
    all_gather x4, waiting for transfers between devices, gather_columns(): return lax.all_gather(piece, 'tgt', axis=1, tiled=True)  24.7 us
    dot_general x2, matrix products, cosine_features(): preact = jnp.dot(samples, omega, preferred_element_type=jnp.float32) + phase  23.8 us
    dot_general x7, matrix products, precise_dot(): return jnp.dot(left_matrix, right_matrix, precision=lax.Precision.HIGHEST)  13.9 us
  transfers between devices with their start and end apart: 8, of which 7 were waited for; matrix products, arithmetic and copies ran while one was open for 10% of the time, Pallas kernels for 8%

profile of v2, /device:TPU:0, one launch (start us, length us, event | category | flops | bytes accessed | tf_op | source)
XLA Modules:
  0.0 430.5 jit_solution(12419764560447765022)
XLA Ops:
  9.2 69.6 %all-gather.24.cloned.1.call-done = bf16[5632,256]{1,0:T(8,128)(2,1)} async-done(((bf16[352,256]{1,0:T(8,128)(2,1)}), bf16[5632,256]{1,0:T(8,128)(2,1)}) %all-gather.24.cloned.1.call-update) | async-done | bytes 2883600 | tf_op jit(solution)/shard_map/all_gather | solution.py:117
  78.8 3.2 slice.8
  82.1 11.9 %fusion.1 = bf16[192,4096]{1,0:T(8,128)(2,1)} fusion(bf16[192,128]{1,0:T(8,128)(2,1)S(1)} %copy-done.12, bf16[128,4096]{1,0:T(8,128)(2,1)S(1)} %copy-done, f32[4096]{0:T(1024)S(1)} %copy-done.13), kind=kOutput, calls=%fused_computation.3 | convolution fusion | flops 202899456 | bytes 2686976 | tf_op jit(solution)/shard_map/dot_general | solution.py:89
  94.0 2.6 convolution_convert_fusion
  98.3 11.9 %fusion.3 = bf16[3072,256]{1,0:T(8,128)(2,1)} fusion(bf16[3072,128]{1,0:T(8,128)(2,1)S(1)} %reshape.13, f32[256]{0:T(256)S(1)} %dynamic_slice.19, bf16[128,4096]{1,0:T(8,128)(2,1)S(1)} %copy-done, s32[]{:T(128)S(6)} %select_n.4), kind=kOutput, calls=%fused_computation.6 | convolution fusion | flops 202899456 | bytes 2425860 | tf_op jit(solution)/shard_map/dot_general | solution.py:89
  110.2 6.8 %fusion.25.gram_ref = f32[512,512]{1,0:T(8,128)} fusion(bf16[4096,512]{1,0:T(8,128)(2,1)} %all-gather.10.cloned.1.call-done), kind=kOutput, calls=%fused_computation.36 | convolution fusion | flops 2147483648 | bytes 5242880 | tf_op jit(solution)/shard_map/dot_general | solution.py:94
  117.0 33.1 %spd_inverse.3 = f32[512,512]{1,0:T(8,128)} custom-call(f32[512,512]{1,0:T(8,128)} %fusion.25.gram_ref), custom_call_target="tpu_custom_call" | custom-call | tf_op jit(solution)/shard_map/spd_inverse/pallas_call | solution.py:81
  150.1 5.5 %all-gather.12.cloned.1.call-done = bf16[3072,256]{1,0:T(8,128)(2,1)} async-done(((bf16[192,256]{1,0:T(8,128)(2,1)}), bf16[3072,256]{1,0:T(8,128)(2,1)}) %all-gather.12.cloned.1.call-update) | async-done | bytes 1572880 | tf_op jit(solution)/shard_map/all_gather | solution.py:117
  158.0 9.0 %all-gather.14.cloned.1.call-done = bf16[3072,512]{1,0:T(8,128)(2,1)} async-done(((bf16[3072,256]{1,0:T(8,128)(2,1)}), bf16[3072,512]{1,0:T(8,128)(2,1)}) %all-gather.14.cloned.1.call-update) | async-done | bytes 3145744 | tf_op jit(solution)/shard_map/all_gather | solution.py:120
  167.1 5.7 %fusion.6.gram_ref = f32[512,512]{1,0:T(8,128)} fusion(f32[512,512]{1,0:T(8,128)S(1)} %copy-done.4, bf16[3072,512]{1,0:T(8,128)(2,1)} %all-gather.14.cloned.1.call-done), kind=kOutput, calls=%fused_computation.11 | convolution fusion | flops 1611137024 | bytes 5242880 | tf_op jit(solution)/shard_map/dot_general | solution.py:94
  172.8 32.9 %spd_inverse.4 = f32[512,512]{1,0:T(8,128)} custom-call(f32[512,512]{1,0:T(8,128)} %fusion.6.gram_ref), custom_call_target="tpu_custom_call" | custom-call | tf_op jit(solution)/shard_map/spd_inverse/pallas_call | solution.py:81
  205.8 3.2 fusion.26
  209.0 2.8 fusion.9
  213.6 61.7 %all-gather.16.cloned.1.call-done = bf16[4096,256]{1,0:T(8,128)(2,1)} async-done(((bf16[256,256]{1,0:T(8,128)(2,1)}), bf16[4096,256]{1,0:T(8,128)(2,1)}) %all-gather.16.cloned.1.call-update) | async-done | bytes 2097168 | tf_op jit(solution)/shard_map/all_gather | solution.py:117
  275.6 12.7 %all-gather.18.cloned.1.call-done = bf16[4096,512]{1,0:T(8,128)(2,1)} async-done(((bf16[4096,256]{1,0:T(8,128)(2,1)}), bf16[4096,512]{1,0:T(8,128)(2,1)}) %all-gather.18.cloned.1.call-update) | async-done | bytes 4194320 | tf_op jit(solution)/shard_map/all_gather | solution.py:120
  288.3 5.9 %fusion.27 = f32[512,512]{1,0:T(8,128)S(1)} fusion(bf16[4096,512]{1,0:T(8,128)(2,1)} %all-gather.18.cloned.1.call-done), kind=kOutput, calls=%fused_computation.38 | convolution fusion | flops 2147483648 | bytes 5242880 | tf_op jit(solution)/shard_map/dot_general | solution.py:94
  294.3 3.4 fusion.28
  300.1 2.9 add_convert_fusion
  305.0 2.7 fusion.11
  307.8 59.3 %all-gather.20.cloned.1.call-done = bf16[3072,256]{1,0:T(8,128)(2,1)} async-done(((bf16[192,256]{1,0:T(8,128)(2,1)}), bf16[3072,256]{1,0:T(8,128)(2,1)}) %all-gather.20.cloned.1.call-update) | async-done | bytes 1572880 | tf_op jit(solution)/shard_map/all_gather | solution.py:117
  369.0 6.9 %fusion.29 = f32[512,512]{1,0:T(8,128)} fusion(bf16[4096,512]{1,0:T(8,128)(2,1)} %copy-done.2), kind=kOutput, calls=%fused_computation.40 | convolution fusion | flops 2147483648 | bytes 5242880 | tf_op jit(solution)/shard_map/dot_general | solution.py:94
  375.8 2.9 all-gather.22.cloned.1.call-done
  378.7 6.0 %fusion.7.gram_ref = f32[512,512]{1,0:T(8,128)} fusion(f32[512,512]{1,0:T(8,128)} %fusion.29, bf16[3072,512]{1,0:T(8,128)(2,1)} %all-gather.22.cloned.1.call-done), kind=kOutput, calls=%fused_computation.12 | convolution fusion | flops 1611137024 | bytes 5242880 | tf_op jit(solution)/shard_map/dot_general | solution.py:94
  384.8 33.2 %spd_inverse.5 = f32[512,512]{1,0:T(8,128)} custom-call(f32[512,512]{1,0:T(8,128)} %fusion.7.gram_ref), custom_call_target="tpu_custom_call" | custom-call | tf_op jit(solution)/shard_map/spd_inverse/pallas_call | solution.py:81
  (62 shorter events, 20.2 us)
Async XLA Ops:
  6.5 75.5 %copy-start = (bf16[128,4096]{1,0:T(8,128)(2,1)S(1)}, bf16[128,4096]{1,0:T(8,128)(2,1)}, u32[]{:S(2)}) copy-start(bf16[128,4096]{1,0:T(8,128)(2,1)} %param.5) | copy-start | bytes 3145732
  6.5 72.3 %all-gather.24.cloned.1.call-start = ((), (), s32[]{:S(2)}) async-start(), calls=%async_computation.7 | async-start | bytes 3063808 | tf_op jit(solution)/shard_map/all_gather | solution.py:117
  9.1 101.0 %all-gather.10.cloned.1.call-start = ((), (), s32[]{:S(2)}) async-start(), calls=%async_computation | async-start | bytes 6291456 | tf_op jit(solution)/shard_map/all_gather | solution.py:120
  78.8 3.3 copy-start.12
  78.8 3.3 copy-start.13
  82.0 12.0 %copy-start.5 = (bf16[16,256,256]{2,1,0:T(8,128)(2,1)S(1)}, bf16[16,256,256]{2,1,0:T(8,128)(2,1)}, u32[]{:S(2)}) copy-start(bf16[16,256,256]{2,1,0:T(8,128)(2,1)} %slice.8) | copy-start | bytes 6291460
  82.0 73.6 %all-gather.12.cloned.1.call-start = ((), (), s32[]{:S(2)}) async-start(), calls=%async_computation.1 | async-start | bytes 1671168 | tf_op jit(solution)/shard_map/all_gather | solution.py:117
  96.7 70.4 %all-gather.14.cloned.1.call-start = ((), (), s32[]{:S(2)}) async-start(), calls=%async_computation.2 | async-start | bytes 4718592 | tf_op jit(solution)/shard_map/all_gather | solution.py:120
  117.0 38.6 %copy-start.11 = (f32[256,256]{1,0:T(8,128)S(1)}, f32[256,256]{1,0:T(8,128)}, u32[]{:S(2)}) copy-start(f32[256,256]{1,0:T(8,128)} %param.7) | copy-start | bytes 786436
  117.0 50.1 %copy-start.4 = (f32[512,512]{1,0:T(8,128)S(1)}, f32[512,512]{1,0:T(8,128)}, u32[]{:S(2)}) copy-start(f32[512,512]{1,0:T(8,128)} %fusion.25.gram_ref) | copy-start | bytes 3145732
  155.6 119.7 %all-gather.16.cloned.1.call-start = ((), (), s32[]{:S(2)}) async-start(), calls=%async_computation.3 | async-start | bytes 2228224 | tf_op jit(solution)/shard_map/all_gather | solution.py:117
  205.8 3.2 copy-start.14
  209.0 2.8 copy-start.8
  213.6 74.7 %all-gather.18.cloned.1.call-start = ((), (), s32[]{:S(2)}) async-start(), calls=%async_computation.4 | async-start | bytes 6291456 | tf_op jit(solution)/shard_map/all_gather | solution.py:120
  275.3 91.7 %all-gather.20.cloned.1.call-start = ((), (), s32[]{:S(2)}) async-start(), calls=%async_computation.5 | async-start | bytes 1671168 | tf_op jit(solution)/shard_map/all_gather | solution.py:117
  288.3 9.4 %copy-start.1 = (bf16[4096,512]{1,0:T(8,128)(2,1)S(1)}, bf16[4096,512]{1,0:T(8,128)(2,1)}, u32[]{:S(2)}) copy-start(bf16[4096,512]{1,0:T(8,128)(2,1)} %all-gather.10.cloned.1.call-done) | copy-start | bytes 12582916
  294.3 3.5 copy-start.6
  297.7 2.4 copy-start.3
  303.0 2.0 copy-start.2
  307.7 71.0 %all-gather.22.cloned.1.call-start = ((), (), s32[]{:S(2)}) async-start(), calls=%async_computation.6 | async-start | bytes 4718592 | tf_op jit(solution)/shard_map/all_gather | solution.py:120
  375.8 42.2 %copy-start.7 = (f32[512,512]{1,0:T(8,128)S(1)}, f32[512,512]{1,0:T(8,128)}, u32[]{:S(2)}) copy-start(f32[512,512]{1,0:T(8,128)} %copy-done.6) | copy-start | bytes 3145732
  384.8 35.5 %copy-start.10 = (f32[256,512]{1,0:T(8,128)S(1)}, f32[256,512]{1,0:T(8,128)}, u32[]{:S(2)}) copy-start(f32[256,512]{1,0:T(8,128)} %fusion.8) | copy-start | bytes 1572868
  418.0 3.3 copy-start.9
Sparse Core Ops, SparseCore 0:
  10.1 68.6 all-gather.23
  82.1 11.4 all-gather.9
  96.8 58.7 all-gather.11
  157.0 10.0 all-gather.13
  213.7 61.5 all-gather.15
  276.7 11.5 all-gather.17
  307.8 59.1 all-gather.19
  368.6 10.1 all-gather.21
